TPU v7x, 32 devices: a whole 2x2x4 slice. The times are simulated.
32 devices in a mesh: task: 16 (over z, x, core), tensor: 2 (over y).
Axes of the slice: x: 2, y: 2, z: 4, core: 2. Of those that a mesh axis runs over, the one named last changes fastest.
Arguments:
- inputs: bfloat16 [2048, 4096], P('task', 'tensor'), may hold values from -6 to 6
- targets: bfloat16 [2048, 4096], P('task', 'tensor'), may hold values from -6 to 6
- queries: bfloat16 [2048, 2048], P('task', 'tensor'), may hold values from -120 to 120
- key_rows: bfloat16 [2048, 2048], P('task', 'tensor'), may hold values from -4 to 4
- value_weight: bfloat16 [4096, 2048], P(None, 'tensor'), may hold values from -0.09375 to 0.09375
- output_weight: bfloat16 [2048, 4096], P('tensor'), may hold values from -0.125 to 0.125
- splits: int32 [16], P('task'), may hold values from 32 to 96
Outputs:
- meta_value: float32 [4096, 2048], P('task', 'tensor')
- meta_output: float32 [2048, 4096], P('tensor', 'task')
Inputs may be any that keep to these rules, and one draw needn't show every extreme that they name: `splits`: support and query parts of every task are both nonempty.
All inputs are finite; a program needn't handle non-finite values.
Results may differ from a plain program's by a relative error of at most 0.025.
Values may be sent and summed in bfloat16 or wider, within the bound.
A program may use at most 128 MiB of HBM per device.

v0:
```python
import jax
import jax.numpy as jnp
from jax import lax
from jax.sharding import PartitionSpec as P

HD = 128
TASK_LEN = 128


step_rate = 0.25


def normed_rows(inputs):
    values = inputs.astype(jnp.float32)
    scale = lax.rsqrt(jnp.mean(values * values, axis=-1, keepdims=True) + 1e-05)
    return (values * scale).astype(jnp.bfloat16)


def attention_probs(queries, key_rows, heads):
    length = queries.shape[0]
    query_f = queries.astype(jnp.float32).reshape(length, heads, -1)
    key_f = key_rows.astype(jnp.float32).reshape(length, heads, -1)
    scores = jnp.einsum("ihd,jhd->hij", query_f, key_f) / jnp.sqrt(jnp.float32(query_f.shape[2]))
    position = jnp.arange(length)
    causal = position[:, None] >= position[None, :]
    scores = jnp.where(causal[None], scores, jnp.float32(-1e30))
    scores = scores - jnp.max(scores, axis=-1, keepdims=True)
    expo = jnp.exp(scores)
    return (expo / jnp.sum(expo, axis=-1, keepdims=True)).astype(jnp.bfloat16)


def local_out(value_mat, output_mat, normed, probs):
    heads = probs.shape[0]
    length = normed.shape[0]
    upper = jnp.dot(
        normed, value_mat.astype(jnp.bfloat16), preferred_element_type=jnp.float32
    ).astype(jnp.bfloat16)
    mixed = jnp.einsum(
        "hij,jhd->ihd",
        probs.astype(jnp.float32),
        upper.astype(jnp.float32).reshape(length, heads, -1),
    )
    mixed = mixed.reshape(length, -1).astype(jnp.bfloat16)
    return jnp.dot(
        mixed, output_mat.astype(jnp.bfloat16), preferred_element_type=jnp.float32
    ).astype(jnp.bfloat16)


def grads_of(value_mat, output_mat, error_term, normed, probs):

    def forward(value_arg, output_arg):
        return local_out(value_arg, output_arg, normed, probs)

    unused, pullback = jax.vjp(forward, value_mat, output_mat)
    return pullback(error_term.astype(jnp.bfloat16))


def combine(term, offset, weight):
    share = lax.psum_scatter(
        term.astype(jnp.bfloat16), "tensor", scatter_dimension=1, tiled=True
    ).astype(jnp.float32)
    return lax.all_gather(
        (weight * (share + offset)).astype(jnp.bfloat16), "tensor", axis=1, tiled=True
    )


def per_device(inputs, targets, queries, key_rows, value_weight, output_weight, splits):
    value_start = value_weight.astype(jnp.float32)
    output_start = output_weight.astype(jnp.float32)
    heads_here = queries.shape[1] // HD
    full_inputs = lax.all_gather(inputs, "tensor", axis=1, tiled=True)
    offset_all = inputs.astype(jnp.float32) - targets.astype(jnp.float32)
    normed_all = normed_rows(full_inputs)
    position = jnp.arange(TASK_LEN)
    total_value = None
    total_output = None
    probs = attention_probs(queries, key_rows, heads_here)
    split = splits[0]
    count_s = split.astype(jnp.float32)
    support = (position < split).astype(jnp.float32)[:, None]
    support_weight = support / count_s
    query_weight = (1.0 - support) / (jnp.float32(TASK_LEN) - count_s)
    part = local_out(value_start, output_start, normed_all, probs)
    error_term = combine(part.astype(jnp.float32), offset_all, support_weight)
    grad_value, grad_output = grads_of(value_start, output_start, error_term, normed_all, probs)
    value_next = value_start - step_rate * grad_value
    output_next = output_start - step_rate * grad_output
    saved_states = [(value_start, output_start, error_term)]
    part_final = local_out(value_next, output_next, normed_all, probs)
    query_term = combine(part_final.astype(jnp.float32), offset_all, query_weight)
    direct_value, direct_output = grads_of(value_next, output_next, query_term, normed_all, probs)
    extra_value = jnp.zeros_like(direct_value)
    extra_output = jnp.zeros_like(direct_output)
    for saved in reversed(saved_states):

        def gradient_map(value_arg, output_arg, error_arg):
            return grads_of(value_arg, output_arg, error_arg, normed_all, probs)

        unused, pull_grads = jax.vjp(gradient_map, saved[0], saved[1], saved[2].astype(jnp.float32))
        second_value, second_output, error_back = pull_grads(
            (-step_rate * direct_value, -step_rate * direct_output)
        )
        out_back = combine(error_back, 0.0, support_weight)

        def forward_map(value_arg, output_arg):
            return local_out(value_arg, output_arg, normed_all, probs)

        unused_out, pull_out = jax.vjp(forward_map, saved[0], saved[1])
        first_value, first_output = pull_out(out_back)
        extra_value = second_value + first_value
        extra_output = second_output + first_output
    total_value = direct_value + extra_value
    total_output = direct_output + extra_output
    total_value, total_output = (
        lax.psum_scatter(
            total_value.astype(jnp.bfloat16), "task", scatter_dimension=0, tiled=True
        ).astype(jnp.float32),
        lax.psum_scatter(
            total_output.astype(jnp.bfloat16), "task", scatter_dimension=1, tiled=True
        ).astype(jnp.float32),
    )
    return (total_value, total_output)


def solution(mesh):
    return jax.shard_map(
        per_device,
        mesh=mesh,
        in_specs=(
            P("task", "tensor"),
            P("task", "tensor"),
            P("task", "tensor"),
            P("task", "tensor"),
            P(None, "tensor"),
            P("tensor", None),
            P("task"),
        ),
        out_specs=(P("task", "tensor"), P("tensor", "task")),
        check_vma=False,
    )
```

profile of v0, /device:TPU:17, one launch (start us, length us, event | category | flops | bytes accessed | tf_op | source)
XLA Modules:
  0.0 462.9 jit_solution(15424022318885126670)
XLA Ops:
  7.2 0.0 all-gather.5.cloned.1.call-start
  7.2 0.7 all-gather.5.cloned.1.call-update
  7.9 0.0 reduce-scatter.6.cloned.1.call-start
  8.0 0.1 copy-done
  8.1 1.3 fusion.53
  9.4 0.1 divide_convert_fusion
  9.5 22.2 %all-gather.5.cloned.1.call-done = bf16[128,4096]{1,0:T(8,128)(2,1)} async-done(((bf16[128,2048]{1,0:T(8,128)(2,1)}), bf16[128,4096]{1,0:T(8,128)(2,1)}) %all-gather.5.cloned.1.call-update) | async-done | bytes 1048592 | tf_op jit(solution)/shard_map/all_gather | solution.py:71
  31.8 1.5 fusion.23
  33.3 5.0 %convolution_convert_fusion.14 = bf16[128,1024]{1,0:T(8,128)(2,1)S(1)} fusion(bf16[4096,1024]{1,0:T(8,128)(2,1)} %param.11, bf16[128,4096]{1,0:T(8,128)(2,1)} %all-gather.5.cloned.1.call-done, f32[128]{0:T(128)S(1)} %add_rsqrt_fusion), kind=kOutput, calls=%fused_computation.46 | convolution fusion | flops 1075445760 | bytes 9699840 | tf_op jit(solution)/shard_map/dot_general | solution.py:35
  38.3 0.2 copy.32
  38.5 0.2 convolution_convert_fusion.13
  38.7 5.6 %convolution_convert_fusion.3 = bf16[128,4096]{1,0:T(8,128)(2,1)} fusion(bf16[128,1024]{0,1:T(8,128)(2,1)S(1)} %bitcast.105, bf16[1024,4096]{1,0:T(8,128)(2,1)} %param.12), kind=kOutput, calls=%fused_computation.24 | convolution fusion | flops 1074266112 | bytes 9699328 | tf_op jit(solution)/shard_map/dot_general | solution.py:44
  44.4 0.0 reduce-scatter.6.cloned.1.call-update
  44.4 0.0 all-gather.7.cloned.1.call-start
  45.2 19.7 %reduce-scatter.6.cloned.1.call-done = bf16[128,2048]{1,0:T(8,128)(2,1)} async-done(((bf16[128,4096]{1,0:T(8,128)(2,1)}), bf16[128,2048]{1,0:T(8,128)(2,1)}) %reduce-scatter.6.cloned.1.call-update) | async-done | bytes 524304 | tf_op jit(solution)/shard_map/reduce_scatter | solution.py:59
  64.9 2.1 multiply_convert_fusion.2
  67.1 0.2 reduce-scatter.8.cloned.1.call-start
  67.3 21.2 %all-gather.7.cloned.1.call-done = bf16[128,4096]{1,0:T(8,128)(2,1)} async-done(((bf16[128,2048]{1,0:T(8,128)(2,1)}), bf16[128,4096]{1,0:T(8,128)(2,1)}) %all-gather.7.cloned.1.call-update) | async-done | bytes 1048592 | tf_op jit(solution)/shard_map/all_gather | solution.py:62
  88.5 6.6 %convolution_convert_fusion.12 = bf16[128,1024]{1,0:T(8,128)(2,1)S(1)} fusion(bf16[128,4096]{1,0:T(8,128)(2,1)} %all-gather.7.cloned.1.call-done, bf16[1024,4096]{1,0:T(8,128)(2,1)} %param.12), kind=kOutput, calls=%fused_computation.44 | convolution fusion | flops 1073872896 | bytes 9699328 | tf_op jit(solution)/shard_map/transpose(jvp())/dot_general | solution.py:44
  95.1 0.2 copy.33
  95.3 0.3 convolution_convert_fusion.11
  95.6 8.0 %fusion.34 = bf16[128,1024]{1,0:T(8,128)(2,1)} fusion(bf16[4096,1024]{1,0:T(8,128)(2,1)} %param.11, bf16[128,1024]{0,1:T(8,128)(2,1)S(1)} %bitcast.123, bf16[128,4096]{1,0:T(8,128)(2,1)S(1)} %copy-done.5, f32[128]{0:T(128)S(1)} %add_rsqrt_fusion), kind=kOutput, calls=%fused_computation.35 | convolution fusion | flops 2175926272 | bytes 9961984 | tf_op jit(solution)/shard_map/dot_general | solution.py:35
  103.6 1.8 copy.34
  105.4 1.2 convolution_convert_fusion.10
  106.6 4.7 %subtract_convert_fusion = bf16[1024,4096]{1,0:T(8,128)(2,1)S(1)} fusion(bf16[1024,4096]{1,0:T(8,128)(2,1)} %param.12, bf16[128,1024]{0,1:T(8,128)(2,1)S(1)} %bitcast.106, bf16[128,4096]{1,0:T(8,128)(2,1)S(1)} %copy-done.6), kind=kOutput, calls=%fused_computation.9 | convolution fusion | flops 1098907648 | bytes 18087936 | tf_op jit(solution)/shard_map/transpose(jvp())/dot_general | solution.py:44
  111.4 3.2 copy-done.2
  114.6 2.3 convolution_convert_fusion.2
  116.9 0.0 all-gather.9.cloned.1.call-start
  117.0 20.5 %reduce-scatter.8.cloned.1.call-done = bf16[128,2048]{1,0:T(8,128)(2,1)} async-done(((bf16[128,4096]{1,0:T(8,128)(2,1)}), bf16[128,2048]{1,0:T(8,128)(2,1)}) %reduce-scatter.8.cloned.1.call-update) | async-done | bytes 524304 | tf_op jit(solution)/shard_map/reduce_scatter | solution.py:59
  137.4 2.3 multiply_convert_fusion.1
  139.7 0.3 reduce-scatter.10.cloned.1.call-start
  140.0 21.2 %all-gather.9.cloned.1.call-done = bf16[128,4096]{1,0:T(8,128)(2,1)} async-done(((bf16[128,2048]{1,0:T(8,128)(2,1)}), bf16[128,4096]{1,0:T(8,128)(2,1)}) %all-gather.9.cloned.1.call-update) | async-done | bytes 1048592 | tf_op jit(solution)/shard_map/all_gather | solution.py:62
  161.1 6.6 %convolution_convert_fusion.9 = bf16[128,1024]{1,0:T(8,128)(2,1)S(1)} fusion(bf16[128,4096]{1,0:T(8,128)(2,1)} %all-gather.9.cloned.1.call-done, bf16[1024,4096]{1,0:T(8,128)(2,1)} %copy-done.2), kind=kOutput, calls=%fused_computation.41 | convolution fusion | flops 1073872896 | bytes 9699328 | tf_op jit(solution)/shard_map/transpose(jvp())/dot_general | solution.py:44
  167.8 0.2 copy.35
  167.9 0.3 convolution_convert_fusion.8
  168.2 2.5 convolution_convert_fusion.1
  170.7 3.2 copy-done.4
  173.9 1.8 fusion.31
  175.8 0.2 copy.37
  176.0 0.2 convolution_convert_fusion.6
  176.2 4.7 %fusion.58 = f32[128,4096]{1,0:T(8,128)S(1)} fusion(bf16[128,1024]{0,1:T(8,128)(2,1)S(1)} %bitcast.111, bf16[1024,4096]{1,0:T(8,128)(2,1)} %param.12), kind=kOutput, calls=%fused_computation.68 | convolution fusion | flops 1073741824 | bytes 10747904 | tf_op jit(solution)/shard_map/transpose(jvp(transpose(jvp())))/dot_general | solution.py:44
  180.9 2.3 convolution_convert_fusion
  183.3 3.2 copy-done.3
  186.5 2.8 fusion.20
  189.4 0.0 all-gather.11.cloned.1.call-start
  189.4 20.5 %reduce-scatter.10.cloned.1.call-done = bf16[128,2048]{1,0:T(8,128)(2,1)} async-done(((bf16[128,4096]{1,0:T(8,128)(2,1)}), bf16[128,2048]{1,0:T(8,128)(2,1)}) %reduce-scatter.10.cloned.1.call-update) | async-done | bytes 524304 | tf_op jit(solution)/shard_map/reduce_scatter | solution.py:59
  209.9 2.0 multiply_convert_fusion
  211.9 0.3 reduce-scatter.14.cloned.1.call-start
  212.2 5.6 %fusion.59 = bf16[1024,4096]{1,0:T(8,128)(2,1)} fusion(bf16[128,1024]{0,1:T(8,128)(2,1)S(1)} %bitcast.112, bf16[128,4096]{1,0:T(8,128)(2,1)S(1)} %copy-done.6), kind=kOutput, calls=%fused_computation.69 | convolution fusion | flops 1073741824 | bytes 9699328 | tf_op jit(solution)/shard_map/transpose(jvp(transpose(jvp())))/dot_general | solution.py:44
  217.8 15.6 %all-gather.11.cloned.1.call-done = bf16[128,4096]{1,0:T(8,128)(2,1)} async-done(((bf16[128,2048]{1,0:T(8,128)(2,1)}), bf16[128,4096]{1,0:T(8,128)(2,1)}) %all-gather.11.cloned.1.call-update) | async-done | bytes 1048592 | tf_op jit(solution)/shard_map/all_gather | solution.py:62
  233.4 9.7 %fusion.4 = bf16[1024,4096]{1,0:T(8,128)(2,1)} fusion(bf16[1024,4096]{1,0:T(8,128)(2,1)} %copy-done.3, bf16[1024,4096]{1,0:T(8,128)(2,1)} %fusion.59, bf16[128,1024]{0,1:T(8,128)(2,1)S(1)} %bitcast.108, bf16[128,4096]{1,0:T(8,128)(2,1)} %all-gather.11.cloned.1.call-done), kind=kOutput, calls=%fused_computation.8 | convolution fusion | flops 1103101952 | bytes 26476544 | tf_op jit(solution)/shard_map/transpose(jvp())/dot_general | solution.py:44
  243.1 0.0 reduce-scatter.12.cloned.1.call-start
  243.1 6.3 %fusion.28 = bf16[128,1024]{1,0:T(8,128)(2,1)S(1)} fusion(bf16[128,4096]{1,0:T(8,128)(2,1)S(1)} %copy-done.6, bf16[1024,4096]{1,0:T(8,128)(2,1)} %copy-done.3), kind=kOutput, calls=%fused_computation.33 | convolution fusion | flops 1086455808 | bytes 9699328 | tf_op jit(solution)/shard_map/transpose(jvp(transpose(jvp())))/dot_general | solution.py:44
  249.5 0.2 copy.36
  249.6 0.3 convolution_convert_fusion.7
  250.0 6.4 %fusion.46 = bf16[4096,1024]{1,0:T(8,128)(2,1)} fusion(bf16[128,1024]{0,1:T(8,128)(2,1)S(1)} %bitcast.115, bf16[128,4096]{1,0:T(8,128)(2,1)S(1)} %copy-done.5, f32[128]{0:T(128)S(1)} %add_rsqrt_fusion), kind=kOutput, calls=%fused_computation.66 | convolution fusion | flops 1075314688 | bytes 9699840 | tf_op jit(solution)/shard_map/transpose(jvp(jvp()))/dot_general | solution.py:35
  256.4 2.9 convolution_convert_fusion.5
  259.3 0.2 copy.38
  259.5 0.3 convolution_convert_fusion.4
  259.8 11.8 %fusion.2 = bf16[4096,1024]{1,0:T(8,128)(2,1)} fusion(bf16[4096,1024]{1,0:T(8,128)(2,1)} %copy-done.4, bf16[4096,1024]{1,0:T(8,128)(2,1)} %fusion.46, bf16[128,1024]{0,1:T(8,128)(2,1)S(1)} %bitcast.113, bf16[128,4096]{1,0:T(8,128)(2,1)S(1)} %copy-done.5, f32[128]{0:T(128)S(1)} %add_rsqrt_fusion), kind=kOutput, calls=%fused_computation.6 | convolution fusion | flops 1104674816 | bytes 26477056 | tf_op jit(solution)/shard_map/transpose(jvp())/dot_general | solution.py:35
  271.6 75.0 %reduce-scatter.14.cloned.1.call-done = bf16[1024,256]{1,0:T(8,128)(2,1)} async-done(((bf16[1024,4096]{1,0:T(8,128)(2,1)}), bf16[1024,256]{1,0:T(8,128)(2,1)}) %reduce-scatter.14.cloned.1.call-update) | async-done | bytes 524304 | tf_op jit(solution)/shard_map/reduce_scatter | solution.py:118
  346.6 2.1 convert_element_type.340
  348.7 105.1 %reduce-scatter.12.cloned.1.call-done = bf16[256,1024]{1,0:T(8,128)(2,1)} async-done(((bf16[4096,1024]{1,0:T(8,128)(2,1)}), bf16[256,1024]{1,0:T(8,128)(2,1)}) %reduce-scatter.12.cloned.1.call-update) | async-done | bytes 524304 | tf_op jit(solution)/shard_map/reduce_scatter | solution.py:115
  453.8 2.1 convert_element_type.334
  (34 shorter events, 0.2 us)
Async XLA Ops:
  7.2 1.0 copy-start
  7.2 24.6 %all-gather.5.cloned.1.call-start = ((), (), s32[]{:S(2)}) async-start(), calls=%async_computation.5 | async-start | bytes 1572864 | tf_op jit(solution)/shard_map/all_gather | solution.py:71
  7.9 57.0 %reduce-scatter.6.cloned.1.call-start = ((), (), s32[]{:S(2)}) async-start(), calls=%async_computation.6 | async-start | bytes 1572864 | tf_op jit(solution)/shard_map/reduce_scatter | solution.py:59
  38.3 26.6 %copy-start.7 = (bf16[128,2048]{1,0:T(8,128)(2,1)S(1)}, bf16[128,2048]{1,0:T(8,128)(2,1)}, u32[]{:S(2)}) copy-start(bf16[128,2048]{1,0:T(8,128)(2,1)} %param.7) | copy-start | bytes 1572868
  38.3 26.6 %copy-start.10 = (bf16[128,2048]{1,0:T(8,128)(2,1)S(1)}, bf16[128,2048]{1,0:T(8,128)(2,1)}, u32[]{:S(2)}) copy-start(bf16[128,2048]{1,0:T(8,128)(2,1)} %param.8) | copy-start | bytes 1572868
  44.4 51.2 %copy-start.5 = (bf16[128,4096]{1,0:T(8,128)(2,1)S(1)}, bf16[128,4096]{1,0:T(8,128)(2,1)}, u32[]{:S(2)}) copy-start(bf16[128,4096]{1,0:T(8,128)(2,1)} %all-gather.5.cloned.1.call-done) | copy-start | bytes 3145732
  44.4 44.1 %all-gather.7.cloned.1.call-start = ((), (), s32[]{:S(2)}) async-start(), calls=%async_computation.7 | async-start | bytes 1572864 | tf_op jit(solution)/shard_map/all_gather | solution.py:62
  67.1 70.4 %reduce-scatter.8.cloned.1.call-start = ((), (), s32[]{:S(2)}) async-start(), calls=%async_computation.8 | async-start | bytes 1572864 | tf_op jit(solution)/shard_map/reduce_scatter | solution.py:59
  95.6 11.0 %copy-start.6 = (bf16[128,4096]{1,0:T(8,128)(2,1)S(1)}, bf16[128,4096]{1,0:T(8,128)(2,1)}, u32[]{:S(2)}) copy-start(bf16[128,4096]{1,0:T(8,128)(2,1)} %all-gather.7.cloned.1.call-done) | copy-start | bytes 3145732
  111.4 3.2 copy-start.2
  116.9 44.2 %all-gather.9.cloned.1.call-start = ((), (), s32[]{:S(2)}) async-start(), calls=%async_computation.9 | async-start | bytes 1572864 | tf_op jit(solution)/shard_map/all_gather | solution.py:62
  139.7 70.2 %reduce-scatter.10.cloned.1.call-start = ((), (), s32[]{:S(2)}) async-start(), calls=%async_computation.10 | async-start | bytes 1572864 | tf_op jit(solution)/shard_map/reduce_scatter | solution.py:59
  170.7 3.2 copy-start.4
  175.9 5.0 %copy-start.9 = (bf16[128,4096]{1,0:T(8,128)(2,1)S(1)}, bf16[128,4096]{1,0:T(8,128)(2,1)}, u32[]{:S(2)}) copy-start(bf16[128,4096]{1,0:T(8,128)(2,1)} %all-gather.9.cloned.1.call-done) | copy-start | bytes 3145732
  183.3 3.2 copy-start.3
  189.4 44.0 %all-gather.11.cloned.1.call-start = ((), (), s32[]{:S(2)}) async-start(), calls=%async_computation.11 | async-start | bytes 1572864 | tf_op jit(solution)/shard_map/all_gather | solution.py:62
  211.9 134.7 %reduce-scatter.14.cloned.1.call-start = ((), (), s32[]{:S(2)}) async-start(), calls=%async_computation.13 | async-start | bytes 8912896 | tf_op jit(solution)/shard_map/reduce_scatter | solution.py:118
  243.1 210.7 %reduce-scatter.12.cloned.1.call-start = ((), (), s32[]{:S(2)}) async-start(), calls=%async_computation.12 | async-start | bytes 8912896 | tf_op jit(solution)/shard_map/reduce_scatter | solution.py:115
  249.4 6.9 %copy-start.8 = (bf16[128,4096]{1,0:T(8,128)(2,1)S(1)}, bf16[128,4096]{1,0:T(8,128)(2,1)}, u32[]{:S(2)}) copy-start(bf16[128,4096]{1,0:T(8,128)(2,1)} %all-gather.11.cloned.1.call-done) | copy-start | bytes 3145732
  249.6 6.8 %slice-start = ((s8[8388608]{0:T(1024)(128)(4,1)}), s8[4194304]{0:T(1024)(128)(4,1)S(1)}, s32[]{:S(2)}) async-start(s8[8388608]{0:T(1024)(128)(4,1)} %bitcast.103), calls=%async_computation.14 | async-start | bytes 8388608
  249.9 6.4 %slice-start.1 = ((s8[8388608]{0:T(1024)(128)(4,1)}), s8[4194304]{0:T(1024)(128)(4,1)S(1)}, s32[]{:S(2)}) async-start(s8[8388608]{0:T(1024)(128)(4,1)} %bitcast.103), calls=%async_computation.15 | async-start | bytes 8388608
  259.8 196.2 %copy-start.1 = (bf16[128,1024]{1,0:T(8,128)(2,1)S(1)}, bf16[128,1024]{1,0:T(8,128)(2,1)}, u32[]{:S(2)}) copy-start(bf16[128,1024]{1,0:T(8,128)(2,1)} %param.10) | copy-start | bytes 786436
Sparse Core Ops, SparseCore 0:
  9.5 22.1 all-gather.4
  44.5 20.3 reduce-scatter.5
  67.2 21.2 all-gather.6
  117.0 20.3 reduce-scatter.7
  139.8 21.2 all-gather.8
  189.5 20.3 reduce-scatter.9
  212.0 21.2 all-gather.10
  243.2 103.3 reduce-scatter.13
  350.7 103.0 reduce-scatter.11
where the time goes:
time: 469 us; the launch traced here: 463 us
  waiting for transfers between devices  322 us (69%)
  matrix products  99.9 us (21%)
  between operations  15.4 us (3%)
  local copies, waits for them, and re-layouts  12.7 us (3%)
  other arithmetic  12.2 us (3%)
    reduce_scatter x1, waiting for transfers between devices, per_device(): lax.psum_scatter(total_value.astype(jnp.bfloat16), 'task', scatter_dimens...  105 us
    reduce_scatter x1, waiting for transfers between devices, per_device(): lax.psum_scatter(total_output.astype(jnp.bfloat16), 'task', scatter_dimen...  75 us
    reduce_scatter x3, waiting for transfers between devices, combine(): lax.psum_scatter(term.astype(jnp.bfloat16), 'tensor', scatter_dimension=1...  60.7 us
    dot_general x12, matrix products, local_out(): jnp.dot(mixed, output_mat.astype(jnp.bfloat16), preferred_element_type=jn...  60.2 us
    all_gather x3, waiting for transfers between devices, combine(): lax.all_gather((weight * (share + offset)).astype(jnp.bfloat16), 'tensor'...  58 us
    dot_general x6, matrix products, local_out(): jnp.dot(normed, value_mat.astype(jnp.bfloat16), preferred_element_type=jn...  35.5 us
    all_gather x1, waiting for transfers between devices, per_device(): full_inputs = lax.all_gather(inputs, 'tensor', axis=1, tiled=True)  22.2 us
    unnamed x26, local copies, waits for them, and re-layouts  9.88 us
  transfers between devices with their start and end apart: 9, of which 9 were waited for; matrix products, arithmetic and copies ran while one was open for 8% of the time, Pallas kernels for 0%

commit v1 on v0

v1 whole, which is shorter than its diff:
```python
import functools

import jax
import jax.numpy as jnp
from jax import lax
from jax.experimental import pallas as pl
from jax.experimental.pallas import tpu as pltpu
from jax.sharding import PartitionSpec as P

HD = 128
BF = jnp.bfloat16
F32 = jnp.float32

step_rate = 0.25


def normed_rows(inputs):
    values = inputs.astype(F32)
    scale = lax.rsqrt(jnp.mean(values * values, axis=-1, keepdims=True) + 1e-05)
    return (values * scale).astype(BF)


def attention_probs(queries, key_rows, heads):
    length = queries.shape[0]
    query_h = queries.reshape(length, heads, -1)
    key_h = key_rows.reshape(length, heads, -1)
    scores = jnp.einsum("ihd,jhd->hij", query_h, key_h, preferred_element_type=F32)
    scores = scores / jnp.sqrt(F32(query_h.shape[2]))
    position = jnp.arange(length)
    causal = position[:, None] >= position[None, :]
    scores = jnp.where(causal[None], scores, F32(-1e30))
    scores = scores - jnp.max(scores, axis=-1, keepdims=True)
    expo = jnp.exp(scores)
    return (expo / jnp.sum(expo, axis=-1, keepdims=True)).astype(BF)


def mm(left, right):
    return jnp.dot(left, right, preferred_element_type=F32)


def mm_nt(left, right):
    return lax.dot_general(left, right, (((1,), (1,)), ((), ())), preferred_element_type=F32)


def mm_tn(left, right):
    return lax.dot_general(left, right, (((0,), (0,)), ((), ())), preferred_element_type=F32)


def mix(probs, rows):
    heads = probs.shape[0]
    split = rows.reshape(rows.shape[0], heads, -1)
    out = jnp.einsum("hij,jhd->ihd", probs, split, preferred_element_type=F32)
    return out.reshape(out.shape[0], -1)


def mix_back(probs, rows):
    heads = probs.shape[0]
    split = rows.reshape(rows.shape[0], heads, -1)
    out = jnp.einsum("hij,ihd->jhd", probs, split, preferred_element_type=F32)
    return out.reshape(out.shape[0], -1)


def group_sum(term, count):
    term = term.astype(BF)
    if count == 1:
        return term.astype(F32)
    if count == 2:
        other = lax.ppermute(term, "tensor", ((0, 1), (1, 0)))
        return term.astype(F32) + other.astype(F32)
    share = lax.psum_scatter(term, "tensor", scatter_dimension=1, tiled=True)
    return lax.all_gather(share, "tensor", axis=1, tiled=True).astype(F32)


def full_rows(inputs, count, index):
    if count != 2:
        return lax.all_gather(inputs, "tensor", axis=1, tiled=True)
    other = lax.ppermute(inputs, "tensor", ((0, 1), (1, 0)))
    low = jnp.where(index == 0, inputs, other)
    high = jnp.where(index == 0, other, inputs)
    return jnp.concatenate([low, high], axis=1)


def gather_kernel(lines, src_ref, out_ref, own_sem, send_sem, line_sem, side_sem, core_sem):
    me = lax.axis_index("task")
    core, side, line = lax.rem(me, 2), lax.rem(me // 2, 2), me // 4

    def place(back, over_side, over_core):
        line_from = lax.rem(line + lines - back, lines)
        side_from = 1 - side if over_side else side
        core_from = 1 - core if over_core else core
        return (line_from * 2 + side_from) * 2 + core_from

    side_peer, core_peer = place(0, True, False), place(0, False, True)
    peers = [place(lines - step, False, False) for step in range(1, lines)] + [side_peer, core_peer]
    barrier = pltpu.get_barrier_semaphore()
    for peer in peers:
        pl.semaphore_signal(
            barrier, inc=1, device_id={"task": peer}, device_id_type=pl.DeviceIdType.MESH
        )
    pl.semaphore_wait(barrier, len(peers))

    started = []

    def send(source, slot, arrival, peer):
        copy = pltpu.make_async_remote_copy(
            src_ref=source,
            dst_ref=out_ref.at[slot],
            send_sem=send_sem.at[len(started)],
            recv_sem=arrival,
            device_id={"task": peer},
            device_id_type=pl.DeviceIdType.MESH,
        )
        copy.start()
        started.append(copy)

    def arrived(slot, arrival, peer):
        pltpu.make_async_remote_copy(
            src_ref=out_ref.at[slot],
            dst_ref=out_ref.at[slot],
            send_sem=send_sem.at[0],
            recv_sem=arrival,
            device_id={"task": peer},
            device_id_type=pl.DeviceIdType.MESH,
        ).wait_recv()

    for step in sorted(range(1, lines), key=lambda step: -min(step, lines - step)):
        send(src_ref, me, line_sem.at[step], peers[step - 1])
    send(src_ref, me, side_sem.at[0], side_peer)
    send(src_ref, me, core_sem.at[0, 0], core_peer)
    own = pltpu.make_async_copy(src_ref, out_ref.at[me], own_sem)
    own.start()
    order = sorted(range(1, lines), key=lambda step: min(step, lines - step))
    for step in order:
        slot = place(step, False, False)
        arrived(slot, line_sem.at[step], side_peer)
        send(out_ref.at[slot], slot, side_sem.at[step], side_peer)
        send(out_ref.at[slot], slot, core_sem.at[step, 0], core_peer)
    for step in [0] + order:
        slot = place(step, True, False)
        arrived(slot, side_sem.at[step], side_peer)
        send(out_ref.at[slot], slot, core_sem.at[step, 1], core_peer)
    for step in [0] + order:
        for over in range(2):
            arrived(place(step, over == 1, True), core_sem.at[step, over], core_peer)
    own.wait()
    for copy in started:
        copy.wait_send()


def gather_by_copies(rows, number):
    count = lax.axis_size("task")
    if count % 4:
        return gather_tokens(rows)
    lines = count // 4
    sends = (lines + 1) + 2 * (lines - 1) + lines
    gathered = pl.pallas_call(
        functools.partial(gather_kernel, lines),
        out_shape=jax.ShapeDtypeStruct((count,) + rows.shape, rows.dtype),
        in_specs=[pl.BlockSpec(memory_space=pltpu.VMEM)],
        out_specs=pl.BlockSpec(memory_space=pltpu.VMEM),
        scratch_shapes=[
            pltpu.SemaphoreType.DMA,
            pltpu.SemaphoreType.DMA((sends,)),
            pltpu.SemaphoreType.DMA((lines,)),
            pltpu.SemaphoreType.DMA((lines,)),
            pltpu.SemaphoreType.DMA((lines, 2)),
        ],
        compiler_params=pltpu.CompilerParams(collective_id=number, has_side_effects=True),
        cost_estimate=pl.CostEstimate(
            flops=0, bytes_accessed=16 * rows.size * rows.dtype.itemsize * count, transcendentals=0
        ),
    )(rows)
    return gathered.reshape(count * rows.shape[0], rows.shape[1])


def gather_tokens(rows):
    return lax.all_gather(rows, "task", axis=0, tiled=True)


def my_columns(rows):
    return lax.all_to_all(rows, "task", split_axis=1, concat_axis=0, tiled=True)


def below(rows, length):
    return jnp.pad(rows, ((0, length - rows.shape[0]), (0, 0)))


def above(rows, length):
    return jnp.pad(rows, ((length - rows.shape[0], 0), (0, 0)))


def make_device(tensor_count):
    def per_device(inputs, targets, queries, key_rows, value_weight, output_weight, splits):
        length = inputs.shape[0]
        low, high = length // 4, 3 * length // 4
        heads = queries.shape[1] // HD
        index = lax.axis_index("tensor")
        normed = normed_rows(full_rows(inputs, tensor_count, index))
        offset_here = inputs.astype(F32) - targets.astype(F32)
        offset = jnp.concatenate(
            [jnp.where(index == block, offset_here, F32(0.0)) for block in range(tensor_count)],
            axis=1,
        )
        probs = attention_probs(queries, key_rows, heads)
        probs_s = probs[:, :high, :high]
        probs_q = probs[:, low:, :]
        split = splits[0]
        count_s = split.astype(F32)
        position = jnp.arange(length)
        support = (position < split).astype(F32)[:, None]
        weight_s = (support / count_s)[:high]
        weight_q = ((1.0 - support) / (F32(length) - count_s))[low:]

        upper = mm(normed, value_weight).astype(BF)
        mixed_s = mix(probs_s, upper[:high]).astype(BF)
        gram = mm_nt(normed, normed).astype(BF)
        mixed_s_all = gather_tokens(mixed_s)
        part_0 = (mm(mixed_s, output_weight) + offset[:high]).astype(BF)
        part_0, normed_sent = lax.optimization_barrier((part_0, normed))
        normed_cols = my_columns(normed_sent)
        error_1 = (weight_s * group_sum(part_0, tensor_count)).astype(BF)

        back_u = mix_back(probs_s, mm_nt(error_1, output_weight).astype(BF)).astype(BF)
        upper_1 = (upper.astype(F32) - step_rate * mm(gram[:, :high], back_u)).astype(BF)
        mixed_q = mix(probs_q, upper_1).astype(BF)
        cross = (-step_rate * mm_nt(mixed_q, mixed_s)).astype(BF)
        part_1 = mm(mixed_q, output_weight) + mm(cross, error_1)
        part_1 = (part_1 + offset[low:]).astype(BF)
        error_2 = (weight_q * group_sum(part_1, tensor_count)).astype(BF)

        errors = (-step_rate * mm_nt(error_2, error_1)).astype(BF)
        back_z1 = (mm_nt(error_2, output_weight) + mm(errors, mixed_s)).astype(BF)
        back_u1 = mix_back(probs_q, back_z1)
        back_u1_b = back_u1.astype(BF)
        back_gram = (-step_rate * mm(gram[:high], back_u1_b)).astype(BF)
        second = mix(probs_s, back_gram).astype(BF)
        error_back = (mm(second, output_weight) + mm_tn(cross, error_2)).astype(BF)
        is_support = (position < split)[:, None]
        left = jnp.where(is_support, below(second, length), above(mixed_q, length))
        errors_both = jnp.where(is_support, below(error_1, length), above(error_2, length))
        error_back, normed_cols, errors_both, left = lax.optimization_barrier(
            (error_back, normed_cols, errors_both, left)
        )
        both_cols = my_columns(errors_both)
        left_all = gather_tokens(left)
        error_sum = group_sum(error_back, tensor_count)
        error_3 = (weight_s * error_sum).astype(BF)
        error_3_cols = my_columns(error_3)

        back_z0 = (mm_nt(error_3, output_weight) + mm_tn(errors, mixed_q)).astype(BF)
        late = mix_back(probs_s, back_z0)
        value_rows = (back_u1 + jnp.pad(late, ((0, length - high), (0, 0)))).astype(BF)
        value_rows_all = gather_by_copies(value_rows, 1)
        total_output = (
            mm_tn(left_all, both_cols)
            + mm_tn(mixed_s_all, error_3_cols)
        )
        total_value = mm_tn(normed_cols, value_rows_all)
        return (total_value, total_output)

    return per_device


def solution(mesh):
    return jax.shard_map(
        make_device(mesh.shape["tensor"]),
        mesh=mesh,
        in_specs=(
            P("task", "tensor"),
            P("task", "tensor"),
            P("task", "tensor"),
            P("task", "tensor"),
            P(None, "tensor"),
            P("tensor", None),
            P("task"),
        ),
        out_specs=(P("task", "tensor"), P("tensor", "task")),
        check_vma=False,
    )
```

time: 469 us -> 243 us (0.52)
  waiting for transfers between devices: 322 us -> 64.3 us
  Pallas kernels: 0 us -> 67.2 us
  matrix products: 99.9 us -> 48.3 us
  starting transfers between devices: 1.01 us -> 27.8 us
    reduce_scatter x5 -> x0, waiting for transfers between devices: 241 us -> none  [the longest x1 105 us: per_device(): lax.psum_scatter(total_value.astype(jnp.bfloat16), 'task', scatter_dimens...]
    all_gather x4 -> x2, waiting for transfers between devices: 80.2 us -> 4.48 us  [gather_tokens(): return lax.all_gather(rows, 'task', axis=0, tiled=True)]
    pallas_call x0 -> x1, Pallas kernels: none -> 67.2 us  [gather_by_copies(): pl.pallas_call(functools.partial(gather_kernel, lines), out_shape=jax.Sha...]
    dot_general x25, matrix products: 98.6 us -> 46.7 us  [the longest x6 19.5 us: mm_nt(): lax.dot_general(left, right, (((1,), (1,)), ((), ())), preferred_element_...]
    ppermute x0 -> x4, waiting for transfers between devices: none -> 46.3 us  [the longest x3 37.8 us: group_sum(): other = lax.ppermute(term, 'tensor', ((0, 1), (1, 0)))]
    all_to_all x0 -> x3, starting transfers between devices: none -> 22.4 us  [my_columns(): return lax.all_to_all(rows, 'task', split_axis=1, concat_axis=0, tiled=True)]
    all_to_all x0 -> x3, waiting for transfers between devices: none -> 13.5 us  [my_columns(): return lax.all_to_all(rows, 'task', split_axis=1, concat_axis=0, tiled=True)]
    unnamed x26 -> x42, local copies, waits for them, and re-layouts: 9.88 us -> 2.51 us
  transfers between devices with their start and end apart: 9 -> 9, of which waited for: 9 -> 6; matrix products, arithmetic and copies ran while one was open for 8% -> 19% of each run, Pallas kernels for 0% -> 28%
where the time goes in v1:
time: 243 us; the launch traced here: 241 us
  Pallas kernels  67.2 us (28%)
  waiting for transfers between devices  64.3 us (26%)
  matrix products  48.3 us (20%)
  starting transfers between devices  27.8 us (11%)
  between operations  15.3 us (6%)
  other arithmetic  9.3 us (4%)
  local copies, waits for them, and re-layouts  8.66 us (4%)
    pallas_call x1, Pallas kernels, gather_by_copies(): pl.pallas_call(functools.partial(gather_kernel, lines), out_shape=jax.Sha...  67.2 us
    ppermute x3, waiting for transfers between devices, group_sum(): other = lax.ppermute(term, 'tensor', ((0, 1), (1, 0)))  37.8 us
    all_to_all x3, starting transfers between devices, my_columns(): return lax.all_to_all(rows, 'task', split_axis=1, concat_axis=0, tiled=True)  22.4 us
    dot_general x6, matrix products, mm_nt(): lax.dot_general(left, right, (((1,), (1,)), ((), ())), preferred_element_...  19.5 us
    dot_general x5, matrix products, mm_tn(): lax.dot_general(left, right, (((0,), (0,)), ((), ())), preferred_element_...  14.1 us
    all_to_all x3, waiting for transfers between devices, my_columns(): return lax.all_to_all(rows, 'task', split_axis=1, concat_axis=0, tiled=True)  13.5 us
    dot_general x8, matrix products, mm(): return jnp.dot(left, right, preferred_element_type=F32)  11.8 us
    ppermute x1, waiting for transfers between devices, full_rows(): other = lax.ppermute(inputs, 'tensor', ((0, 1), (1, 0)))  8.54 us
  transfers between devices with their start and end apart: 9, of which 6 were waited for; matrix products, arithmetic and copies ran while one was open for 19% of the time, Pallas kernels for 28%

profile of v1, /device:TPU:17, one launch (start us, length us, event | category | flops | bytes accessed | tf_op | source)
XLA Modules:
  0.0 240.8 jit_solution(13662327327215683227)
XLA Ops:
  7.2 1.3 collective-permute-start
  8.5 1.6 fusion.64
  10.1 0.2 divide_convert_fusion
  10.3 1.4 fusion.26
  11.7 8.5 %collective-permute-done = bf16[128,2048]{1,0:T(8,128)(2,1)S(1)} collective-permute-done((bf16[128,2048]{1,0:T(8,128)(2,1)}, bf16[128,2048]{1,0:T(8,128)(2,1)S(1)}, u32[]{:S(2)}, u32[]{:S(2)}) %collective-permute-start) | collective-permute-done | bytes 524320 | tf_op jit(solution)/shard_map/ppermute | solution.py:77
  20.3 0.1 broadcast_select_fusion.1
  20.3 0.3 fusion.5
  20.7 0.3 fusion.6
  21.0 1.3 convolution_convert_fusion
  22.3 0.2 convolution_convert_fusion.3
  22.5 0.5 copy-done.10
  23.0 1.3 slice-done.1
  24.3 1.5 fusion.2
  25.9 1.3 collective-permute-start.1
  27.9 0.4 convolution_convert_fusion.6
  28.4 15.2 %collective-permute-done.1 = bf16[96,4096]{1,0:T(8,128)(2,1)} collective-permute-done((bf16[96,4096]{1,0:T(8,128)(2,1)S(1)}, bf16[96,4096]{1,0:T(8,128)(2,1)}, u32[]{:S(2)}, u32[]{:S(2)}) %collective-permute-start.1) | collective-permute-done | bytes 786464 | tf_op jit(solution)/shard_map/ppermute | solution.py:68
  43.6 1.6 multiply_convert_fusion.2
  45.3 6.2 %fusion.20 = bf16[12,8,8,128]{3,2,1,0:T(8,128)(2,1)S(1)} fusion(bf16[96,4096]{1,0:T(8,128)(2,1)S(1)} %multiply_convert_fusion.2, bf16[1024,4096]{1,0:T(8,128)(2,1)} %param.12), kind=kOutput, calls=%fused_computation.44 | convolution fusion | flops 805404672 | bytes 9371648 | tf_op jit(solution)/shard_map/dot_general | solution.py:42
  51.5 0.3 fusion.17
  51.8 0.2 fusion.16
  52.0 0.2 convolution_convert_fusion.2
  52.2 1.5 fusion.63
  53.8 0.2 fusion.25
  54.0 1.3 fusion.3
  55.3 1.3 collective-permute-start.2
  56.6 0.1 slice_bitcast_fusion.2
  56.6 1.1 copy.112
  57.7 8.4 %all-to-all-start = ((bf16[128,16,256]{2,0,1:T(8,128)(2,1)}), bf16[128,16,256]{2,0,1:T(8,128)(2,1)}, u32[]{:S(2)}, u32[]{:S(2)}) async-start(bf16[128,16,256]{2,0,1:T(8,128)(2,1)} %bitcast.162), calls=%async_computation | async-start | bytes 2097152 | tf_op jit(solution)/shard_map/all_to_all | solution.py:181
  66.1 0.2 all-gather.3.cloned.1.call-start
  66.3 0.7 copy_bitcast_fusion.5
  67.0 5.3 %collective-permute-done.2 = bf16[96,4096]{1,0:T(8,128)(2,1)S(1)} collective-permute-done((bf16[96,4096]{1,0:T(8,128)(2,1)}, bf16[96,4096]{1,0:T(8,128)(2,1)S(1)}, u32[]{:S(2)}, u32[]{:S(2)}) %collective-permute-start.2) | collective-permute-done | bytes 786464 | tf_op jit(solution)/shard_map/ppermute | solution.py:68
  72.3 1.4 multiply_convert_fusion.1
  73.7 0.4 fusion.24
  74.1 0.6 copy-done.15
  74.7 0.2 fusion.61
  74.9 6.1 %fusion.22 = bf16[12,8,8,128]{3,2,1,0:T(8,128)(2,1)S(1)} fusion(f32[96,1024]{1,0:T(8,128)S(1)} %fusion.61, bf16[96,4096]{1,0:T(8,128)(2,1)S(1)} %multiply_convert_fusion.1, bf16[1024,4096]{1,0:T(8,128)(2,1)} %param.12), kind=kOutput, calls=%fused_computation.46 | convolution fusion | flops 805502976 | bytes 9764864 | tf_op jit(solution)/shard_map/dot_general | solution.py:42
  81.0 0.3 fusion.41
  81.3 0.2 copy.42
  81.5 0.9 fusion.19
  82.4 0.2 fusion.18
  82.7 1.8 pad_select_fusion.1
  84.4 4.8 %fusion.60 = f32[96,4096]{1,0:T(8,128)S(1)} fusion(bf16[1024,4096]{1,0:T(8,128)(2,1)} %param.12, bf16[8,12,8,128]{3,2,1,0:T(8,128)(2,1)S(1)} %fusion.18), kind=kOutput, calls=%fused_computation.110 | convolution fusion | flops 805306368 | bytes 10158080 | tf_op jit(solution)/shard_map/dot_general | solution.py:38
  89.3 1.3 fusion.4
  90.6 1.3 pad_select_fusion
  91.9 0.0 all-gather.3.cloned.1.call-update
  91.9 0.0 all-gather.5.cloned.1.call-start
  92.0 0.7 copy_bitcast_fusion.6
  92.7 2.4 copy.111
  95.1 8.9 %all-to-all-start.1 = ((bf16[128,16,256]{2,0,1:T(8,128)(2,1)}), bf16[128,16,256]{2,0,1:T(8,128)(2,1)}, u32[]{:S(2)}, u32[]{:S(2)}) async-start(bf16[128,16,256]{2,0,1:T(8,128)(2,1)} %bitcast.161), calls=%async_computation.1 | async-start | bytes 2097152 | tf_op jit(solution)/shard_map/all_to_all | solution.py:181
  104.0 1.3 collective-permute-start.3
  105.3 0.2 fusion.62
  105.5 17.2 %collective-permute-done.3 = bf16[96,4096]{1,0:T(8,128)(2,1)S(1)} collective-permute-done((bf16[96,4096]{1,0:T(8,128)(2,1)S(1)}, bf16[96,4096]{1,0:T(8,128)(2,1)S(1)}, u32[]{:S(2)}, u32[]{:S(2)}) %collective-permute-start.3) | collective-permute-done | bytes 786464 | tf_op jit(solution)/shard_map/ppermute | solution.py:68
  122.8 0.3 multiply_convert_fusion
  123.0 1.0 copy.113
  124.0 13.5 %all-to-all-done.1 = bf16[128,16,256]{2,0,1:T(8,128)(2,1)} async-done(((bf16[128,16,256]{2,0,1:T(8,128)(2,1)}), bf16[128,16,256]{2,0,1:T(8,128)(2,1)}, u32[]{:S(2)}, u32[]{:S(2)}) %all-to-all-start.1) | async-done | bytes 1048608 | tf_op jit(solution)/shard_map/all_to_all | solution.py:181
  137.5 5.1 %all-to-all-start.2 = ((bf16[96,16,256]{2,0,1:T(8,128)(2,1)}), bf16[96,16,256]{2,0,1:T(8,128)(2,1)S(1)}, u32[]{:S(2)}, u32[]{:S(2)}) async-start(bf16[96,16,256]{2,0,1:T(8,128)(2,1)} %bitcast.163), calls=%async_computation.2 | async-start | bytes 1572864 | tf_op jit(solution)/shard_map/all_to_all | solution.py:181
  142.6 6.1 %fusion.21 = bf16[12,8,8,128]{3,2,1,0:T(8,128)(2,1)S(1)} fusion(f32[96,1024]{1,0:T(8,128)S(1)} %fusion.62, bf16[96,4096]{1,0:T(8,128)(2,1)S(1)} %multiply_convert_fusion, bf16[1024,4096]{1,0:T(8,128)(2,1)} %param.12), kind=kOutput, calls=%fused_computation.45 | convolution fusion | flops 805502976 | bytes 9764864 | tf_op jit(solution)/shard_map/dot_general | solution.py:42
  148.7 0.3 convolution_bitcast_fusion
  149.0 0.8 add_convert_fusion.src_ref
  149.7 67.2 %shard_map.86 = bf16[16,128,1024]{2,1,0:T(8,128)(2,1)} custom-call(bf16[128,1024]{1,0:T(8,128)(2,1)} %add_convert_fusion.src_ref), custom_call_target="tpu_custom_call" | custom-call | bytes 67108864 | tf_op jit(solution)/shard_map/pallas_call | solution.py:156
  216.9 4.8 %fusion.69 = f32[256,1024]{1,0:T(8,128)} fusion(bf16[2048,256]{1,0:T(8,128)(2,1)} %bitcast.11, bf16[2048,1024]{1,0:T(8,128)(2,1)} %bitcast.176), kind=kOutput, calls=%fused_computation.115 | convolution fusion | flops 1073741824 | bytes 6291456 | tf_op jit(solution)/shard_map/dot_general | solution.py:46
  221.7 3.9 %fusion.70 = f32[1024,256]{1,0:T(8,128)S(1)} fusion(bf16[2048,1024]{1,0:T(8,128)(2,1)} %all-gather.3.cloned.1.call-done, bf16[2048,256]{1,0:T(8,128)(2,1)} %bitcast.16), kind=kOutput, calls=%fused_computation.116 | convolution fusion | flops 1073741824 | bytes 6291456 | tf_op jit(solution)/shard_map/dot_general | solution.py:46
  225.6 4.5 %all-gather.5.cloned.1.call-done = bf16[1536,1024]{1,0:T(8,128)(2,1)} async-done(((bf16[96,1024]{1,0:T(8,128)(2,1)}), bf16[1536,1024]{1,0:T(8,128)(2,1)}) %all-gather.5.cloned.1.call-update) | async-done | bytes 3145744 | tf_op jit(solution)/shard_map/all_gather | solution.py:177
  230.1 3.9 %convolution_add_fusion.3 = f32[1024,256]{1,0:T(8,128)} fusion(f32[1024,256]{1,0:T(8,128)S(1)} %fusion.70, bf16[1536,1024]{1,0:T(8,128)(2,1)} %all-gather.5.cloned.1.call-done, bf16[1536,256]{1,0:T(8,128)(2,1)S(1)} %bitcast.180), kind=kOutput, calls=%fused_computation.19 | convolution fusion | flops 805568512 | bytes 6029312 | tf_op jit(solution)/shard_map/dot_general | solution.py:46
  (53 shorter events, 0.2 us)
Async XLA Ops:
  7.2 1.4 copy-start
  7.2 3.1 %copy-start.9 = (bf16[128,2048]{1,0:T(8,128)(2,1)S(1)}, bf16[128,2048]{1,0:T(8,128)(2,1)}, u32[]{:S(2)}) copy-start(bf16[128,2048]{1,0:T(8,128)(2,1)} %param.7) | copy-start | bytes 1572868
  7.2 13.1 %collective-permute-start = (bf16[128,2048]{1,0:T(8,128)(2,1)}, bf16[128,2048]{1,0:T(8,128)(2,1)S(1)}, u32[]{:S(2)}, u32[]{:S(2)}) collective-permute-start(bf16[128,2048]{1,0:T(8,128)(2,1)} %param.7), channel_id=1, source_target_pairs={{0,1},{1,0},{2,3},{3,2},{4,5},{5,4},{6,7},{7,6},{8,9},{9,8},{10,11... | collective-permute-start | bytes 1572872 | tf_op jit(solution)/shard_map/ppermute | solution.py:77
  10.3 12.0 %copy-start.4 = (bf16[8,128,128]{2,1,0:T(8,128)(2,1)}, bf16[8,128,128]{2,1,0:T(8,128)(2,1)S(1)}, u32[]{:S(2)}) copy-start(bf16[8,128,128]{2,1,0:T(8,128)(2,1)S(1)} %divide_convert_fusion) | copy-start | bytes 786436
  10.3 10.6 %copy-start.1 = (bf16[4096,1024]{1,0:T(8,128)(2,1)S(1)}, bf16[4096,1024]{1,0:T(8,128)(2,1)}, u32[]{:S(2)}) copy-start(bf16[4096,1024]{1,0:T(8,128)(2,1)} %param.11) | copy-start | bytes 25165828
  11.7 11.3 %copy-start.2 = (f32[128,2048]{1,0:T(8,128)}, f32[128,2048]{1,0:T(8,128)S(1)}, u32[]{:S(2)}) copy-start(f32[128,2048]{1,0:T(8,128)S(1)} %get-tuple-element.15) | copy-start | bytes 3145732
  20.7 2.3 slice-start
  21.0 3.4 %slice-start.1 = ((s8[8388608]{0:T(1024)(128)(4,1)}), s8[4194304]{0:T(1024)(128)(4,1)S(1)}, s32[]{:S(2)}) async-start(s8[8388608]{0:T(1024)(128)(4,1)} %bitcast.170), calls=%async_computation.6 | async-start | bytes 8388608
  22.3 0.7 copy-start.10
  25.8 2.5 %copy-start.8 = (bf16[96,4096]{1,0:T(8,128)(2,1)}, bf16[96,4096]{1,0:T(8,128)(2,1)S(1)}, u32[]{:S(2)}) copy-start(bf16[96,4096]{1,0:T(8,128)(2,1)S(1)} %fusion.2) | copy-start | bytes 2359300
  25.9 17.7 %collective-permute-start.1 = (bf16[96,4096]{1,0:T(8,128)(2,1)S(1)}, bf16[96,4096]{1,0:T(8,128)(2,1)}, u32[]{:S(2)}, u32[]{:S(2)}) collective-permute-start(bf16[96,4096]{1,0:T(8,128)(2,1)S(1)} %fusion.2), channel_id=1, source_target_pairs={{0,1},{1,0},{2,3},{3,2},{4,5},{5,4},{6,7},{7,6},{8,9},{9,8},{10,11... | collective-permute-start | bytes 2359304 | tf_op jit(solution)/shard_map/ppermute | solution.py:68
  27.9 24.3 %slice-start.2 = ((s8[8388608]{0:T(1024)(128)(4,1)}), s8[4194304]{0:T(1024)(128)(4,1)S(1)}, s32[]{:S(2)}) async-start(s8[8388608]{0:T(1024)(128)(4,1)} %bitcast.172), calls=%async_computation.7 | async-start | bytes 8388608
  28.3 23.4 %copy-start.12 = (bf16[128,128]{1,0:T(8,128)(2,1)}, bf16[128,128]{1,0:T(8,128)(2,1)S(1)}, u32[]{:S(2)}) copy-start(bf16[128,128]{1,0:T(8,128)(2,1)S(1)} %convolution_convert_fusion.6) | copy-start | bytes 98308
  45.2 6.3 %copy-start.5 = (bf16[8,128,128]{2,1,0:T(8,128)(2,1)S(1)}, bf16[8,128,128]{2,1,0:T(8,128)(2,1)}, u32[]{:S(2)}) copy-start(bf16[8,128,128]{2,1,0:T(8,128)(2,1)} %copy-done.4) | copy-start | bytes 786436
  45.2 6.5 %copy-start.11 = (bf16[128,1024]{1,0:T(8,128)(2,1)S(1)}, bf16[128,1024]{1,0:T(8,128)(2,1)}, u32[]{:S(2)}) copy-start(bf16[128,1024]{1,0:T(8,128)(2,1)} %copy-done.10) | copy-start | bytes 786436
  45.2 7.0 %slice-start.3 = ((s8[8388608]{0:T(1024)(128)(4,1)}), s8[4194304]{0:T(1024)(128)(4,1)S(1)}, s32[]{:S(2)}) async-start(s8[8388608]{0:T(1024)(128)(4,1)} %bitcast.172), calls=%async_computation.8 | async-start | bytes 8388608
  52.2 1.7 copy-start.3
  54.0 1.3 copy-start.13
  55.3 17.0 %collective-permute-start.2 = (bf16[96,4096]{1,0:T(8,128)(2,1)}, bf16[96,4096]{1,0:T(8,128)(2,1)S(1)}, u32[]{:S(2)}, u32[]{:S(2)}) collective-permute-start(bf16[96,4096]{1,0:T(8,128)(2,1)} %fusion.3), channel_id=1, source_target_pairs={{0,1},{1,0},{2,3},{3,2},{4,5},{5,4},{6,7},{7,6},{8,9},{9,8},{10,11... | collective-permute-start | bytes 2359304 | tf_op jit(solution)/shard_map/ppermute | solution.py:68
  57.7 34.2 %all-to-all-start = ((bf16[128,16,256]{2,0,1:T(8,128)(2,1)}), bf16[128,16,256]{2,0,1:T(8,128)(2,1)}, u32[]{:S(2)}, u32[]{:S(2)}) async-start(bf16[128,16,256]{2,0,1:T(8,128)(2,1)} %bitcast.162), calls=%async_computation | async-start | bytes 2097152 | tf_op jit(solution)/shard_map/all_to_all | solution.py:181
  66.1 155.6 %all-gather.3.cloned.1.call-start = ((), (), s32[]{:S(2)}) async-start(), calls=%async_computation.3 | async-start | bytes 4456448 | tf_op jit(solution)/shard_map/all_gather | solution.py:177
  74.1 0.6 copy-start.15
  74.9 6.1 %copy-start.6 = (bf16[8,128,128]{2,1,0:T(8,128)(2,1)S(1)}, bf16[8,128,128]{2,1,0:T(8,128)(2,1)}, u32[]{:S(2)}) copy-start(bf16[8,128,128]{2,1,0:T(8,128)(2,1)} %copy-done.4) | copy-start | bytes 786436
  84.4 4.8 %copy-start.14 = (bf16[96,96]{1,0:T(8,128)(2,1)S(1)}, bf16[96,96]{1,0:T(8,128)(2,1)}, u32[]{:S(2)}) copy-start(bf16[96,96]{1,0:T(8,128)(2,1)} %copy-done.13) | copy-start | bytes 55300
  91.9 138.2 %all-gather.5.cloned.1.call-start = ((), (), s32[]{:S(2)}) async-start(), calls=%async_computation.4 | async-start | bytes 3342336 | tf_op jit(solution)/shard_map/all_gather | solution.py:177
  92.7 11.3 %copy-start.7 = (bf16[96,4096]{1,0:T(8,128)(2,1)S(1)}, bf16[96,4096]{1,0:T(8,128)(2,1)}, u32[]{:S(2)}) copy-start(bf16[96,4096]{1,0:T(8,128)(2,1)} %fusion.4) | copy-start | bytes 2359300
  92.7 12.6 %copy-start.16 = (bf16[96,96]{1,0:T(8,128)(2,1)S(1)}, bf16[96,96]{1,0:T(8,128)(2,1)}, u32[]{:S(2)}) copy-start(bf16[96,96]{1,0:T(8,128)(2,1)} %copy-done.15) | copy-start | bytes 55300
  95.1 42.4 %all-to-all-start.1 = ((bf16[128,16,256]{2,0,1:T(8,128)(2,1)}), bf16[128,16,256]{2,0,1:T(8,128)(2,1)}, u32[]{:S(2)}, u32[]{:S(2)}) async-start(bf16[128,16,256]{2,0,1:T(8,128)(2,1)} %bitcast.161), calls=%async_computation.1 | async-start | bytes 2097152 | tf_op jit(solution)/shard_map/all_to_all | solution.py:181
  104.0 18.8 %collective-permute-start.3 = (bf16[96,4096]{1,0:T(8,128)(2,1)S(1)}, bf16[96,4096]{1,0:T(8,128)(2,1)S(1)}, u32[]{:S(2)}, u32[]{:S(2)}) collective-permute-start(bf16[96,4096]{1,0:T(8,128)(2,1)S(1)} %copy-done.7), channel_id=1, source_target_pairs={{0,1},{1,0},{2,3},{3,2},{4,5},{5,4},{6,7},{7,6},{8,9},{9,8},{10,11... | collective-permute-start | bytes 2359304 | tf_op jit(solution)/shard_map/ppermute | solution.py:68
  137.5 88.1 %all-to-all-start.2 = ((bf16[96,16,256]{2,0,1:T(8,128)(2,1)}), bf16[96,16,256]{2,0,1:T(8,128)(2,1)S(1)}, u32[]{:S(2)}, u32[]{:S(2)}) async-start(bf16[96,16,256]{2,0,1:T(8,128)(2,1)} %bitcast.163), calls=%async_computation.2 | async-start | bytes 1572864 | tf_op jit(solution)/shard_map/all_to_all | solution.py:181
Sparse Core Ops, SparseCore 0:
  92.0 79.4 all-gather.2
  173.8 56.2 all-gather.4

commit v2 on v1

--- a/solution.py
+++ b/solution.py
@@ -242,6 +242,7 @@
             (error_back, normed_cols, errors_both, left)
         )
         both_cols = my_columns(errors_both)
+        left, mixed_s_all = lax.optimization_barrier((left, mixed_s_all))
         left_all = gather_tokens(left)
         error_sum = group_sum(error_back, tensor_count)
         error_3 = (weight_s * error_sum).astype(BF)

time: 243 us -> 236 us (0.971)
  starting transfers between devices: 27.8 us -> 25 us
  waiting for transfers between devices: 64.3 us -> 61.5 us
    all_gather x2, waiting for transfers between devices: 4.48 us -> 0.01 us  [gather_tokens(): return lax.all_gather(rows, 'task', axis=0, tiled=True)]
    all_to_all x3, starting transfers between devices: 22.4 us -> 19.5 us  [my_columns(): return lax.all_to_all(rows, 'task', split_axis=1, concat_axis=0, tiled=True)]
  transfers between devices with their start and end apart: 9 -> 9, of which waited for: 6 -> 6; matrix products, arithmetic and copies ran while one was open for 19% -> 23% of each run, Pallas kernels for 28% -> 29%
where the time goes in v2:
time: 236 us; the launch traced here: 235 us
  Pallas kernels  68 us (29%)
  waiting for transfers between devices  61.5 us (26%)
  matrix products  48.1 us (20%)
  starting transfers between devices  25 us (11%)
  between operations  15.3 us (6%)
  local copies, waits for them, and re-layouts  8.72 us (4%)
  other arithmetic  8.38 us (4%)
    pallas_call x1, Pallas kernels, gather_by_copies(): pl.pallas_call(functools.partial(gather_kernel, lines), out_shape=jax.Sha...  68 us
    ppermute x3, waiting for transfers between devices, group_sum(): other = lax.ppermute(term, 'tensor', ((0, 1), (1, 0)))  37.8 us
    all_to_all x3, starting transfers between devices, my_columns(): return lax.all_to_all(rows, 'task', split_axis=1, concat_axis=0, tiled=True)  19.5 us
    dot_general x6, matrix products, mm_nt(): lax.dot_general(left, right, (((1,), (1,)), ((), ())), preferred_element_...  19.5 us
    all_to_all x3, waiting for transfers between devices, my_columns(): return lax.all_to_all(rows, 'task', split_axis=1, concat_axis=0, tiled=True)  15.8 us
    dot_general x5, matrix products, mm_tn(): lax.dot_general(left, right, (((0,), (0,)), ((), ())), preferred_element_...  13.9 us
    dot_general x8, matrix products, mm(): return jnp.dot(left, right, preferred_element_type=F32)  11.8 us
    ppermute x1, waiting for transfers between devices, full_rows(): other = lax.ppermute(inputs, 'tensor', ((0, 1), (1, 0)))  7.85 us
  transfers between devices with their start and end apart: 9, of which 6 were waited for; matrix products, arithmetic and copies ran while one was open for 23% of the time, Pallas kernels for 29%

profile of v2, /device:TPU:17, one launch (start us, length us, event | category | flops | bytes accessed | tf_op | source)
XLA Modules:
  0.0 235.0 jit_solution(8156788030210971994)
XLA Ops:
  7.2 0.0 all-gather.3.cloned.1.call-start
  7.2 1.3 collective-permute-start
  9.2 1.6 fusion.64
  10.8 0.2 divide_convert_fusion
  11.1 1.4 fusion.26
  12.5 7.9 %collective-permute-done = bf16[128,2048]{1,0:T(8,128)(2,1)S(1)} collective-permute-done((bf16[128,2048]{1,0:T(8,128)(2,1)}, bf16[128,2048]{1,0:T(8,128)(2,1)S(1)}, u32[]{:S(2)}, u32[]{:S(2)}) %collective-permute-start) | collective-permute-done | bytes 524320 | tf_op jit(solution)/shard_map/ppermute | solution.py:77
  20.3 0.1 broadcast_select_fusion.1
  20.4 0.3 fusion.5
  20.7 0.3 fusion.6
  21.0 1.3 convolution_convert_fusion
  22.3 0.2 convolution_convert_fusion.3
  22.5 0.5 copy-done.10
  23.0 1.3 slice-done.1
  24.4 1.5 fusion.2
  25.9 1.3 collective-permute-start.1
  27.2 0.7 copy_bitcast_fusion.6
  28.0 0.4 convolution_convert_fusion.6
  28.4 15.2 %collective-permute-done.1 = bf16[96,4096]{1,0:T(8,128)(2,1)} collective-permute-done((bf16[96,4096]{1,0:T(8,128)(2,1)S(1)}, bf16[96,4096]{1,0:T(8,128)(2,1)}, u32[]{:S(2)}, u32[]{:S(2)}) %collective-permute-start.1) | collective-permute-done | bytes 786464 | tf_op jit(solution)/shard_map/ppermute | solution.py:68
  43.6 1.6 multiply_convert_fusion.2
  45.3 6.2 %fusion.20 = bf16[12,8,8,128]{3,2,1,0:T(8,128)(2,1)S(1)} fusion(bf16[96,4096]{1,0:T(8,128)(2,1)S(1)} %multiply_convert_fusion.2, bf16[1024,4096]{1,0:T(8,128)(2,1)} %param.12), kind=kOutput, calls=%fused_computation.44 | convolution fusion | flops 805404672 | bytes 9371648 | tf_op jit(solution)/shard_map/dot_general | solution.py:42
  51.6 0.3 fusion.17
  51.8 0.2 fusion.16
  52.1 0.2 convolution_convert_fusion.2
  52.3 1.5 fusion.63
  53.8 0.2 fusion.25
  54.1 1.3 fusion.3
  55.4 1.2 collective-permute-start.2
  56.6 0.1 slice_bitcast_fusion.2
  56.7 1.1 copy.112
  57.8 8.4 %all-to-all-start = ((bf16[128,16,256]{2,0,1:T(8,128)(2,1)}), bf16[128,16,256]{2,0,1:T(8,128)(2,1)}, u32[]{:S(2)}, u32[]{:S(2)}) async-start(bf16[128,16,256]{2,0,1:T(8,128)(2,1)} %bitcast.162), calls=%async_computation | async-start | bytes 2097152 | tf_op jit(solution)/shard_map/all_to_all | solution.py:181
  66.2 0.2 all-gather.5.cloned.1.call-start
  66.4 0.7 copy_bitcast_fusion.5
  67.1 5.3 %collective-permute-done.2 = bf16[96,4096]{1,0:T(8,128)(2,1)S(1)} collective-permute-done((bf16[96,4096]{1,0:T(8,128)(2,1)}, bf16[96,4096]{1,0:T(8,128)(2,1)S(1)}, u32[]{:S(2)}, u32[]{:S(2)}) %collective-permute-start.2) | collective-permute-done | bytes 786464 | tf_op jit(solution)/shard_map/ppermute | solution.py:68
  72.4 1.4 multiply_convert_fusion.1
  73.8 0.4 fusion.24
  74.1 0.6 copy-done.16
  74.7 0.2 fusion.61
  75.0 6.2 %fusion.22 = bf16[12,8,8,128]{3,2,1,0:T(8,128)(2,1)S(1)} fusion(f32[96,1024]{1,0:T(8,128)S(1)} %fusion.61, bf16[96,4096]{1,0:T(8,128)(2,1)S(1)} %multiply_convert_fusion.1, bf16[1024,4096]{1,0:T(8,128)(2,1)} %param.12), kind=kOutput, calls=%fused_computation.46 | convolution fusion | flops 805502976 | bytes 9764864 | tf_op jit(solution)/shard_map/dot_general | solution.py:42
  81.1 0.3 fusion.41
  81.4 0.2 copy.42
  81.6 0.9 fusion.19
  82.6 0.2 fusion.18
  82.8 0.8 pad_select_fusion.1
  83.7 4.8 %fusion.60 = f32[96,4096]{1,0:T(8,128)S(1)} fusion(bf16[1024,4096]{1,0:T(8,128)(2,1)} %param.12, bf16[8,12,8,128]{3,2,1,0:T(8,128)(2,1)S(1)} %fusion.18), kind=kOutput, calls=%fused_computation.110 | convolution fusion | flops 805306368 | bytes 10158080 | tf_op jit(solution)/shard_map/dot_general | solution.py:38
  88.5 1.3 fusion.4
  89.8 1.3 pad_select_fusion
  91.1 2.9 %all-to-all-done = bf16[128,16,256]{2,0,1:T(8,128)(2,1)} async-done(((bf16[128,16,256]{2,0,1:T(8,128)(2,1)}), bf16[128,16,256]{2,0,1:T(8,128)(2,1)}, u32[]{:S(2)}, u32[]{:S(2)}) %all-to-all-start) | async-done | bytes 1048608 | tf_op jit(solution)/shard_map/all_to_all | solution.py:181
  94.0 0.0 all-gather.5.cloned.1.call-update
  94.1 2.4 %copy.111 = bf16[16,16,8,256]{3,2,0,1:T(8,128)(2,1)} copy(bf16[16,16,8,256]{3,2,1,0:T(8,128)(2,1)} %bitcast.177) | data formatting | bytes 2097152 | tf_op jit(solution)/shard_map/all_to_all | solution.py:181
  96.4 6.0 %all-to-all-start.1 = ((bf16[128,16,256]{2,0,1:T(8,128)(2,1)}), bf16[128,16,256]{2,0,1:T(8,128)(2,1)}, u32[]{:S(2)}, u32[]{:S(2)}) async-start(bf16[128,16,256]{2,0,1:T(8,128)(2,1)} %bitcast.161), calls=%async_computation.1 | async-start | bytes 2097152 | tf_op jit(solution)/shard_map/all_to_all | solution.py:181
  102.4 1.3 collective-permute-start.3
  103.8 0.2 fusion.62
  104.0 17.3 %collective-permute-done.3 = bf16[96,4096]{1,0:T(8,128)(2,1)S(1)} collective-permute-done((bf16[96,4096]{1,0:T(8,128)(2,1)S(1)}, bf16[96,4096]{1,0:T(8,128)(2,1)S(1)}, u32[]{:S(2)}, u32[]{:S(2)}) %collective-permute-start.3) | collective-permute-done | bytes 786464 | tf_op jit(solution)/shard_map/ppermute | solution.py:68
  121.3 0.3 multiply_convert_fusion
  121.6 1.0 copy.113
  122.6 12.9 %all-to-all-done.1 = bf16[128,16,256]{2,0,1:T(8,128)(2,1)} async-done(((bf16[128,16,256]{2,0,1:T(8,128)(2,1)}), bf16[128,16,256]{2,0,1:T(8,128)(2,1)}, u32[]{:S(2)}, u32[]{:S(2)}) %all-to-all-start.1) | async-done | bytes 1048608 | tf_op jit(solution)/shard_map/all_to_all | solution.py:181
  135.5 5.1 %all-to-all-start.2 = ((bf16[96,16,256]{2,0,1:T(8,128)(2,1)}), bf16[96,16,256]{2,0,1:T(8,128)(2,1)S(1)}, u32[]{:S(2)}, u32[]{:S(2)}) async-start(bf16[96,16,256]{2,0,1:T(8,128)(2,1)} %bitcast.163), calls=%async_computation.2 | async-start | bytes 1572864 | tf_op jit(solution)/shard_map/all_to_all | solution.py:181
  140.6 6.1 %fusion.21 = bf16[12,8,8,128]{3,2,1,0:T(8,128)(2,1)S(1)} fusion(f32[96,1024]{1,0:T(8,128)S(1)} %fusion.62, bf16[96,4096]{1,0:T(8,128)(2,1)S(1)} %multiply_convert_fusion, bf16[1024,4096]{1,0:T(8,128)(2,1)} %param.12), kind=kOutput, calls=%fused_computation.45 | convolution fusion | flops 805502976 | bytes 9764864 | tf_op jit(solution)/shard_map/dot_general | solution.py:42
  146.7 0.3 convolution_bitcast_fusion
  147.0 0.8 add_convert_fusion.src_ref
  147.7 68.0 %shard_map.86 = bf16[16,128,1024]{2,1,0:T(8,128)(2,1)} custom-call(bf16[128,1024]{1,0:T(8,128)(2,1)} %add_convert_fusion.src_ref), custom_call_target="tpu_custom_call" | custom-call | bytes 67108864 | tf_op jit(solution)/shard_map/pallas_call | solution.py:156
  215.7 4.8 %fusion.69 = f32[256,1024]{1,0:T(8,128)} fusion(bf16[2048,256]{1,0:T(8,128)(2,1)} %bitcast.11, bf16[2048,1024]{1,0:T(8,128)(2,1)} %bitcast.176), kind=kOutput, calls=%fused_computation.115 | convolution fusion | flops 1073741824 | bytes 6291456 | tf_op jit(solution)/shard_map/dot_general | solution.py:46
  220.5 3.8 %fusion.70 = f32[1024,256]{1,0:T(8,128)S(1)} fusion(bf16[2048,1024]{1,0:T(8,128)(2,1)} %all-gather.5.cloned.1.call-done, bf16[2048,256]{1,0:T(8,128)(2,1)} %bitcast.16), kind=kOutput, calls=%fused_computation.116 | convolution fusion | flops 1073741824 | bytes 6291456 | tf_op jit(solution)/shard_map/dot_general | solution.py:46
  224.3 3.9 %convolution_add_fusion.3 = f32[1024,256]{1,0:T(8,128)} fusion(f32[1024,256]{1,0:T(8,128)S(1)} %fusion.70, bf16[1536,1024]{1,0:T(8,128)(2,1)} %all-gather.3.cloned.1.call-done, bf16[1536,256]{1,0:T(8,128)(2,1)S(1)} %bitcast.180), kind=kOutput, calls=%fused_computation.19 | convolution fusion | flops 805568512 | bytes 6029312 | tf_op jit(solution)/shard_map/dot_general | solution.py:46
  (55 shorter events, 0.2 us)
Async XLA Ops:
  7.2 2.0 copy-start
  7.2 3.9 %copy-start.9 = (bf16[128,2048]{1,0:T(8,128)(2,1)S(1)}, bf16[128,2048]{1,0:T(8,128)(2,1)}, u32[]{:S(2)}) copy-start(bf16[128,2048]{1,0:T(8,128)(2,1)} %param.7) | copy-start | bytes 1572868
  7.2 86.8 %all-gather.3.cloned.1.call-start = ((), (), s32[]{:S(2)}) async-start(), calls=%async_computation.3 | async-start | bytes 3342336 | tf_op jit(solution)/shard_map/all_gather | solution.py:177
  7.2 13.1 %collective-permute-start = (bf16[128,2048]{1,0:T(8,128)(2,1)}, bf16[128,2048]{1,0:T(8,128)(2,1)S(1)}, u32[]{:S(2)}, u32[]{:S(2)}) collective-permute-start(bf16[128,2048]{1,0:T(8,128)(2,1)} %param.7), channel_id=1, source_target_pairs={{0,1},{1,0},{2,3},{3,2},{4,5},{5,4},{6,7},{7,6},{8,9},{9,8},{10,11... | collective-permute-start | bytes 1572872 | tf_op jit(solution)/shard_map/ppermute | solution.py:77
  11.0 11.3 %copy-start.4 = (bf16[8,128,128]{2,1,0:T(8,128)(2,1)}, bf16[8,128,128]{2,1,0:T(8,128)(2,1)S(1)}, u32[]{:S(2)}) copy-start(bf16[8,128,128]{2,1,0:T(8,128)(2,1)S(1)} %divide_convert_fusion) | copy-start | bytes 786436
  11.1 9.9 %copy-start.1 = (bf16[4096,1024]{1,0:T(8,128)(2,1)S(1)}, bf16[4096,1024]{1,0:T(8,128)(2,1)}, u32[]{:S(2)}) copy-start(bf16[4096,1024]{1,0:T(8,128)(2,1)} %param.11) | copy-start | bytes 25165828
  12.5 10.6 %copy-start.2 = (f32[128,2048]{1,0:T(8,128)}, f32[128,2048]{1,0:T(8,128)S(1)}, u32[]{:S(2)}) copy-start(f32[128,2048]{1,0:T(8,128)S(1)} %get-tuple-element.19) | copy-start | bytes 3145732
  20.7 2.3 slice-start
  21.0 3.4 %slice-start.1 = ((s8[8388608]{0:T(1024)(128)(4,1)}), s8[4194304]{0:T(1024)(128)(4,1)S(1)}, s32[]{:S(2)}) async-start(s8[8388608]{0:T(1024)(128)(4,1)} %bitcast.170), calls=%async_computation.6 | async-start | bytes 8388608
  22.3 0.7 copy-start.10
  25.9 2.5 %copy-start.8 = (bf16[96,4096]{1,0:T(8,128)(2,1)}, bf16[96,4096]{1,0:T(8,128)(2,1)S(1)}, u32[]{:S(2)}) copy-start(bf16[96,4096]{1,0:T(8,128)(2,1)S(1)} %fusion.2) | copy-start | bytes 2359300
  25.9 17.7 %collective-permute-start.1 = (bf16[96,4096]{1,0:T(8,128)(2,1)S(1)}, bf16[96,4096]{1,0:T(8,128)(2,1)}, u32[]{:S(2)}, u32[]{:S(2)}) collective-permute-start(bf16[96,4096]{1,0:T(8,128)(2,1)S(1)} %fusion.2), channel_id=1, source_target_pairs={{0,1},{1,0},{2,3},{3,2},{4,5},{5,4},{6,7},{7,6},{8,9},{9,8},{10,11... | collective-permute-start | bytes 2359304 | tf_op jit(solution)/shard_map/ppermute | solution.py:68
  28.0 24.3 %slice-start.2 = ((s8[8388608]{0:T(1024)(128)(4,1)}), s8[4194304]{0:T(1024)(128)(4,1)S(1)}, s32[]{:S(2)}) async-start(s8[8388608]{0:T(1024)(128)(4,1)} %bitcast.172), calls=%async_computation.7 | async-start | bytes 8388608
  28.4 23.4 %copy-start.13 = (bf16[128,128]{1,0:T(8,128)(2,1)}, bf16[128,128]{1,0:T(8,128)(2,1)S(1)}, u32[]{:S(2)}) copy-start(bf16[128,128]{1,0:T(8,128)(2,1)S(1)} %convolution_convert_fusion.6) | copy-start | bytes 98308
  45.3 6.3 %copy-start.5 = (bf16[8,128,128]{2,1,0:T(8,128)(2,1)S(1)}, bf16[8,128,128]{2,1,0:T(8,128)(2,1)}, u32[]{:S(2)}) copy-start(bf16[8,128,128]{2,1,0:T(8,128)(2,1)} %copy-done.4) | copy-start | bytes 786436
  45.3 6.5 %copy-start.11 = (bf16[128,1024]{1,0:T(8,128)(2,1)S(1)}, bf16[128,1024]{1,0:T(8,128)(2,1)}, u32[]{:S(2)}) copy-start(bf16[128,1024]{1,0:T(8,128)(2,1)} %copy-done.10) | copy-start | bytes 786436
  45.3 7.0 %slice-start.3 = ((s8[8388608]{0:T(1024)(128)(4,1)}), s8[4194304]{0:T(1024)(128)(4,1)S(1)}, s32[]{:S(2)}) async-start(s8[8388608]{0:T(1024)(128)(4,1)} %bitcast.172), calls=%async_computation.8 | async-start | bytes 8388608
  52.3 1.7 copy-start.3
  54.0 1.3 copy-start.14
  55.4 17.0 %collective-permute-start.2 = (bf16[96,4096]{1,0:T(8,128)(2,1)}, bf16[96,4096]{1,0:T(8,128)(2,1)S(1)}, u32[]{:S(2)}, u32[]{:S(2)}) collective-permute-start(bf16[96,4096]{1,0:T(8,128)(2,1)} %fusion.3), channel_id=1, source_target_pairs={{0,1},{1,0},{2,3},{3,2},{4,5},{5,4},{6,7},{7,6},{8,9},{9,8},{10,11... | collective-permute-start | bytes 2359304 | tf_op jit(solution)/shard_map/ppermute | solution.py:68
  57.8 36.2 %all-to-all-start = ((bf16[128,16,256]{2,0,1:T(8,128)(2,1)}), bf16[128,16,256]{2,0,1:T(8,128)(2,1)}, u32[]{:S(2)}, u32[]{:S(2)}) async-start(bf16[128,16,256]{2,0,1:T(8,128)(2,1)} %bitcast.162), calls=%async_computation | async-start | bytes 2097152 | tf_op jit(solution)/shard_map/all_to_all | solution.py:181
  66.2 154.3 %all-gather.5.cloned.1.call-start = ((), (), s32[]{:S(2)}) async-start(), calls=%async_computation.4 | async-start | bytes 4456448 | tf_op jit(solution)/shard_map/all_gather | solution.py:177
  74.1 0.6 copy-start.16
  74.9 6.2 %copy-start.6 = (bf16[8,128,128]{2,1,0:T(8,128)(2,1)S(1)}, bf16[8,128,128]{2,1,0:T(8,128)(2,1)}, u32[]{:S(2)}) copy-start(bf16[8,128,128]{2,1,0:T(8,128)(2,1)} %copy-done.4) | copy-start | bytes 786436
  81.1 1.7 copy-start.12
  83.7 4.8 %copy-start.15 = (bf16[96,96]{1,0:T(8,128)(2,1)S(1)}, bf16[96,96]{1,0:T(8,128)(2,1)}, u32[]{:S(2)}) copy-start(bf16[96,96]{1,0:T(8,128)(2,1)} %copy-done.14) | copy-start | bytes 55300
  94.0 8.4 %copy-start.7 = (bf16[96,4096]{1,0:T(8,128)(2,1)S(1)}, bf16[96,4096]{1,0:T(8,128)(2,1)}, u32[]{:S(2)}) copy-start(bf16[96,4096]{1,0:T(8,128)(2,1)} %fusion.4) | copy-start | bytes 2359300
  94.0 9.7 %copy-start.17 = (bf16[96,96]{1,0:T(8,128)(2,1)S(1)}, bf16[96,96]{1,0:T(8,128)(2,1)}, u32[]{:S(2)}) copy-start(bf16[96,96]{1,0:T(8,128)(2,1)} %copy-done.16) | copy-start | bytes 55300
  96.4 39.1 %all-to-all-start.1 = ((bf16[128,16,256]{2,0,1:T(8,128)(2,1)}), bf16[128,16,256]{2,0,1:T(8,128)(2,1)}, u32[]{:S(2)}, u32[]{:S(2)}) async-start(bf16[128,16,256]{2,0,1:T(8,128)(2,1)} %bitcast.161), calls=%async_computation.1 | async-start | bytes 2097152 | tf_op jit(solution)/shard_map/all_to_all | solution.py:181
  102.4 18.9 %collective-permute-start.3 = (bf16[96,4096]{1,0:T(8,128)(2,1)S(1)}, bf16[96,4096]{1,0:T(8,128)(2,1)S(1)}, u32[]{:S(2)}, u32[]{:S(2)}) collective-permute-start(bf16[96,4096]{1,0:T(8,128)(2,1)S(1)} %copy-done.7), channel_id=1, source_target_pairs={{0,1},{1,0},{2,3},{3,2},{4,5},{5,4},{6,7},{7,6},{8,9},{9,8},{10,11... | collective-permute-start | bytes 2359304 | tf_op jit(solution)/shard_map/ppermute | solution.py:68
  135.5 88.8 %all-to-all-start.2 = ((bf16[96,16,256]{2,0,1:T(8,128)(2,1)}), bf16[96,16,256]{2,0,1:T(8,128)(2,1)S(1)}, u32[]{:S(2)}, u32[]{:S(2)}) async-start(bf16[96,16,256]{2,0,1:T(8,128)(2,1)} %bitcast.163), calls=%async_computation.2 | async-start | bytes 1572864 | tf_op jit(solution)/shard_map/all_to_all | solution.py:181
Sparse Core Ops, SparseCore 0:
  28.1 50.6 all-gather.2
  94.2 78.3 all-gather.4
